TPU v7x, 32 devices: a whole 2x2x4 slice. The times are simulated.
32 devices in a mesh: groups: 2 (over x), dp: 16 (over z, y, core).
Axes of the slice: x: 2, y: 2, z: 4, core: 2. Of those that a mesh axis runs over, the one named last changes fastest.
Arguments:
- batch_counts: int32 [32], P(('groups', 'dp')), parts along dimension 0, may hold values from 1 to 4, 32 in all
- attn_out: bfloat16 [128, 7168], P(('groups', 'dp')), parts along dimension 0, may hold values from -6 to 6
- residual_in: bfloat16 [128, 7168], P(('groups', 'dp')), parts along dimension 0, may hold values from -64 to 64
- norm_gain: float32 [7168], replicated, may hold values from 0.5 to 1.5
- w_gate_up: bfloat16 [2, 18432, 7168], P(None, 'dp'), may hold values from -0.0625 to 0.0625
- w_down: bfloat16 [18432, 7168], P(None, 'dp'), may hold values from -0.046875 to 0.046875
- next_gain: float32 [7168], replicated, may hold values from 0.5 to 1.5
Outputs:
- hidden_out: bfloat16 [128, 7168], P(('groups', 'dp')), parts along dimension 0
- normed_out: bfloat16 [128, 7168], P(('groups', 'dp')), parts along dimension 0
There are 2 independent parts, one for each index of `groups`. A program takes and returns all parts, laid end to end along the dimension named above; an argument that names none is the same for every part. Nothing has to cross between parts.
Inputs may be any that keep to these rules, and one draw needn't show every extreme that they name: Rank r's occupied rows are its first batch_counts[r] slots; the counts sum to exactly 32, and some rank holds 4.
All inputs are finite; a program needn't handle non-finite values. No bound on the sum of `batch_counts` on one device may be relied on, other than what follows from the above.
Results may differ from a plain program's by a relative error of at most 0.0045.
Values may be sent and summed in bfloat16 or wider, within the bound.
A program may use at most 128 MiB of HBM per device.

v0:
```python
import jax
import jax.numpy as jnp
from jax import lax
from jax.sharding import PartitionSpec as P

EPSILON = 1e-06


def normalize(values, weight_gain):
    mean_square = jnp.mean(values * values, axis=-1, keepdims=True)
    return values * lax.rsqrt(mean_square + EPSILON) * weight_gain


def mlp_hidden(picked_rows, w_gate_up):
    both_parts = jnp.einsum(
        "rd,gfd->grf", picked_rows, w_gate_up, preferred_element_type=jnp.float32
    )
    return (jax.nn.silu(both_parts[0]) * both_parts[1]).astype(jnp.bfloat16)


def on_device(batch_counts, attn_out, residual_in, norm_gain, w_gate_up, w_down, next_gain):
    slot_count = attn_out.shape[0]
    occupied = lax.broadcasted_iota(jnp.int32, (slot_count, 1), 0) < batch_counts[0]
    summed = residual_in.astype(jnp.float32) + attn_out.astype(jnp.float32)
    normed_in = normalize(summed, norm_gain).astype(jnp.bfloat16)
    hidden_rows = mlp_hidden(lax.all_gather(normed_in, "dp", axis=0, tiled=True), w_gate_up)
    down_cols = jnp.dot(
        lax.all_gather(hidden_rows, "dp", axis=1, tiled=True),
        w_down,
        preferred_element_type=jnp.float32,
    )
    mlp_out = lax.all_to_all(
        down_cols.astype(jnp.bfloat16), "dp", split_axis=0, concat_axis=1, tiled=True
    )
    updated = summed + mlp_out.astype(jnp.float32)
    hidden_out = jnp.where(occupied, updated, 0.0).astype(jnp.bfloat16)
    normed_out = jnp.where(occupied, normalize(updated, next_gain), 0.0).astype(jnp.bfloat16)
    return (hidden_out, normed_out)


def solution(mesh):
    placed = (
        P(("groups", "dp")),
        P(("groups", "dp"), None),
        P(("groups", "dp"), None),
        P(),
        P(None, "dp", None),
        P(None, "dp"),
        P(),
    )
    return jax.shard_map(
        on_device,
        mesh=mesh,
        in_specs=placed,
        out_specs=(P(("groups", "dp"), None), P(("groups", "dp"), None)),
        check_vma=False,
    )
```

profile of v0, /device:TPU:0, one launch (start us, length us, event | category | flops | bytes accessed | tf_op | source)
XLA Modules:
  0.0 121.2 jit_solution(10895494308429920050)
XLA Ops:
  7.2 0.0 all-gather.3.cloned.1.call-start
  7.2 1.0 multiply_reduce_fusion.1
  8.2 0.9 fusion.3
  9.2 25.9 %all-gather = bf16[16,4,7168]{2,1,0:T(4,128)(2,1)S(1)} all-gather(bf16[1,4,7168]{2,1,0:T(4,128)(2,1)S(1)} %fusion.3), channel_id=1, replica_groups=mesh['groups'=2,'dp'=16] {'dp'}, dimensions={0}, use_global_device_ids=true | all-gather | bytes 974848 | tf_op jit(solution)/shard_map/all_gather | solution.py:26
  35.1 0.2 reshape.35
  35.3 14.8 %convolution_bitcast_fusion = f32[2,64,1152]{2,1,0:T(8,128)S(1)} fusion(bf16[64,7168,1]{1,0,2:T(8,128)(2,1)S(1)} %reshape.35, bf16[2,1152,7168]{2,1,0:T(8,128)(2,1)} %param.11), kind=kOutput, calls=%fused_computation | convolution fusion | flops 2113929216 | bytes 34537472 | tf_op jit(solution)/shard_map/rd,gfd->grf/dot_general | solution.py:15
  50.1 0.0 copy-start
  50.1 0.0 copy-start.1
  50.1 0.0 copy-start.2
  50.1 0.7 fusion.1
  50.9 0.0 all-gather.3.cloned.1.call-update
  51.5 39.5 %all-gather.3.cloned.1.call-done = bf16[64,18432]{1,0:T(8,128)(2,1)} async-done(((bf16[64,1152]{1,0:T(8,128)(2,1)}), bf16[64,18432]{1,0:T(8,128)(2,1)}) %all-gather.3.cloned.1.call-update) | async-done | bytes 2359312 | tf_op jit(solution)/shard_map/all_gather | solution.py:28
  91.0 11.2 %convolution_convert_fusion = bf16[64,448]{1,0:T(8,128)(2,1)S(1)} fusion(bf16[64,18432]{1,0:T(8,128)(2,1)} %all-gather.3.cloned.1.call-done, bf16[18432,448]{0,1:T(8,128)(2,1)} %param.12), kind=kOutput, calls=%fused_computation.1 | convolution fusion | flops 1056993280 | bytes 18931712 | tf_op jit(solution)/shard_map/dot_general | solution.py:27
  102.2 0.6 all_to_all.10
  102.9 3.5 %all-to-all-start = ((bf16[16,4,448]{2,1,0:T(4,128)(2,1)}), bf16[16,4,448]{2,1,0:T(4,128)(2,1)S(1)}, u32[]{:S(2)}, u32[]{:S(2)}) async-start(bf16[16,4,448]{2,1,0:T(4,128)(2,1)} %all_to_all.10), calls=%async_computation | async-start | bytes 131072 | tf_op jit(solution)/shard_map/all_to_all | solution.py:32
  106.4 6.8 %all-to-all-done = bf16[16,4,448]{2,1,0:T(4,128)(2,1)S(1)} async-done(((bf16[16,4,448]{2,1,0:T(4,128)(2,1)}), bf16[16,4,448]{2,1,0:T(4,128)(2,1)S(1)}, u32[]{:S(2)}, u32[]{:S(2)}) %all-to-all-start) | async-done | bytes 57376 | tf_op jit(solution)/shard_map/all_to_all | solution.py:32
  113.3 0.1 reshape.32
  113.4 0.0 copy-done
  113.4 0.0 copy-done.1
  113.4 0.2 multiply_reduce_fusion
  113.6 0.0 copy-done.2
  113.6 0.8 select_convert_fusion
  (5 shorter events, 0.1 us)
Async XLA Ops:
  7.2 83.8 %all-gather.3.cloned.1.call-start = ((), (), s32[]{:S(2)}) async-start(), calls=%async_computation.1 | async-start | bytes 2506752 | tf_op jit(solution)/shard_map/all_gather | solution.py:28
  50.1 63.3 %copy-start = (bf16[4,7168]{1,0:T(4,128)(2,1)S(1)}, bf16[4,7168]{1,0:T(4,128)(2,1)}, u32[]{:S(2)}) copy-start(bf16[4,7168]{1,0:T(4,128)(2,1)} %param.8) | copy-start | bytes 172036
  50.1 63.3 %copy-start.1 = (bf16[4,7168]{1,0:T(4,128)(2,1)S(1)}, bf16[4,7168]{1,0:T(4,128)(2,1)}, u32[]{:S(2)}) copy-start(bf16[4,7168]{1,0:T(4,128)(2,1)} %param.9) | copy-start | bytes 172036
  50.1 63.5 %copy-start.2 = (f32[7168]{0:T(1024)S(1)}, f32[7168]{0:T(1024)}, u32[]{:S(2)}) copy-start(f32[7168]{0:T(1024)} %param.13) | copy-start | bytes 86020
  102.9 10.4 %all-to-all-start = ((bf16[16,4,448]{2,1,0:T(4,128)(2,1)}), bf16[16,4,448]{2,1,0:T(4,128)(2,1)S(1)}, u32[]{:S(2)}, u32[]{:S(2)}) async-start(bf16[16,4,448]{2,1,0:T(4,128)(2,1)} %all_to_all.10), calls=%async_computation | async-start | bytes 131072 | tf_op jit(solution)/shard_map/all_to_all | solution.py:32
Sparse Core Ops, SparseCore 0:
  51.0 39.9 all-gather.2
where the time goes:
time: 122 us; the launch traced here: 121 us
  waiting for transfers between devices  46.3 us (38%)
  matrix products  26 us (21%)
  blocking collectives  25.9 us (21%)
  between operations  14.8 us (12%)
  other arithmetic  3.69 us (3%)
  starting transfers between devices  3.53 us (3%)
    all_gather x1, waiting for transfers between devices, on_device(): lax.all_gather(hidden_rows, 'dp', axis=1, tiled=True)  39.5 us
    all_gather x1, blocking collectives, on_device(): lax.all_gather(normed_in, 'dp', axis=0, tiled=True)  25.9 us
    dot_general x1, matrix products, mlp_hidden(): jnp.einsum('rd,gfd->grf', picked_rows, w_gate_up, preferred_element_type=...  14.8 us
    dot_general x1, matrix products, on_device(): jnp.dot(lax.all_gather(hidden_rows, 'dp', axis=1, tiled=True), w_down, pr...  11.2 us
    all_to_all x1, waiting for transfers between devices, on_device(): lax.all_to_all(down_cols.astype(jnp.bfloat16), 'dp', split_axis=0, concat...  6.85 us
    all_to_all x1, starting transfers between devices, on_device(): lax.all_to_all(down_cols.astype(jnp.bfloat16), 'dp', split_axis=0, concat...  3.49 us
  transfers between devices with their start and end apart: 2, of which 2 were waited for; matrix products, arithmetic and copies ran while one was open for 0% of the time, Pallas kernels for 0%

commit v1 on v0

--- a/solution.py
+++ b/solution.py
@@ -25,7 +25,9 @@
     normed_in = normalize(summed, norm_gain).astype(jnp.bfloat16)
     hidden_rows = mlp_hidden(lax.all_gather(normed_in, "dp", axis=0, tiled=True), w_gate_up)
     down_cols = jnp.dot(
-        lax.all_gather(hidden_rows, "dp", axis=1, tiled=True),
+        jnp.concatenate(
+            lax.all_to_all(jnp.stack([hidden_rows] * lax.axis_size("dp")), "dp", 0, 0), axis=1
+        ),
         w_down,
         preferred_element_type=jnp.float32,
     )

time: 122 us -> 130 us (1.066)
  between operations: 14.8 us -> 1.39 us
  starting transfers between devices: 3.53 us -> 16 us
  waiting for transfers between devices: 46.3 us -> 51.7 us
  local copies, waits for them, and re-layouts: 1.04 us -> 6.17 us
    all_to_all x0 -> x1, waiting for transfers between devices: none -> 44.8 us  [on_device(): lax.all_to_all(jnp.stack([hidden_rows] * lax.axis_size('dp')), 'dp', 0, 0)]
    all_gather x1 -> x0, waiting for transfers between devices: 39.5 us -> none  [on_device(): lax.all_gather(hidden_rows, 'dp', axis=1, tiled=True)]
    all_to_all x1, starting transfers between devices: 3.49 us -> 12.2 us  [on_device(): lax.all_to_all(down_cols.astype(jnp.bfloat16), 'dp', split_axis=0, concat...]
    all_to_all x0 -> x1, starting transfers between devices: none -> 3.72 us  [on_device(): lax.all_to_all(jnp.stack([hidden_rows] * lax.axis_size('dp')), 'dp', 0, 0)]
    reshape x0 -> x1, local copies, waits for them, and re-layouts: none -> 1.97 us  [on_device(): jnp.concatenate(lax.all_to_all(jnp.stack([hidden_rows] * lax.axis_size('d...]
    another operation x0 -> x1, local copies, waits for them, and re-layouts: none -> 1.74 us  [on_device(): jnp.stack([hidden_rows] * lax.axis_size('dp'))]
    unnamed x7 -> x9, local copies, waits for them, and re-layouts: 0.22 us -> 1.65 us
where the time goes in v1:
time: 130 us; the launch traced here: 129 us
  waiting for transfers between devices  51.7 us (40%)
  blocking collectives  25.9 us (20%)
  matrix products  25.3 us (19%)
  starting transfers between devices  16 us (12%)
  local copies, waits for them, and re-layouts  6.17 us (5%)
  other arithmetic  3.03 us (2%)
  between operations  1.39 us (1%)
    all_to_all x1, waiting for transfers between devices, on_device(): lax.all_to_all(jnp.stack([hidden_rows] * lax.axis_size('dp')), 'dp', 0, 0)  44.8 us
    all_gather x1, blocking collectives, on_device(): lax.all_gather(normed_in, 'dp', axis=0, tiled=True)  25.9 us
    dot_general x1, matrix products, mlp_hidden(): jnp.einsum('rd,gfd->grf', picked_rows, w_gate_up, preferred_element_type=...  14.8 us
    all_to_all x1, starting transfers between devices, on_device(): lax.all_to_all(down_cols.astype(jnp.bfloat16), 'dp', split_axis=0, concat...  12.2 us
    dot_general x1, matrix products, on_device(): jnp.dot(jnp.concatenate(lax.all_to_all(jnp.stack([hidden_rows] * lax.axis...  10.5 us
    all_to_all x1, waiting for transfers between devices, on_device(): lax.all_to_all(down_cols.astype(jnp.bfloat16), 'dp', split_axis=0, concat...  6.88 us
    all_to_all x1, starting transfers between devices, on_device(): lax.all_to_all(jnp.stack([hidden_rows] * lax.axis_size('dp')), 'dp', 0, 0)  3.72 us
  transfers between devices with their start and end apart: 2, of which 2 were waited for; matrix products, arithmetic and copies ran while one was open for 0% of the time, Pallas kernels for 0%

profile of v1, /device:TPU:0, one launch (start us, length us, event | category | flops | bytes accessed | tf_op | source)
XLA Modules:
  0.0 129.5 jit_solution(14458107057408925450)
XLA Ops:
  0.6 1.0 multiply_reduce_fusion.1
  1.7 0.9 fusion.3
  2.6 25.9 %all-gather = bf16[16,4,7168]{2,1,0:T(4,128)(2,1)S(1)} all-gather(bf16[1,4,7168]{2,1,0:T(4,128)(2,1)S(1)} %fusion.3), channel_id=1, replica_groups=mesh['groups'=2,'dp'=16] {'dp'}, dimensions={0}, use_global_device_ids=true | all-gather | bytes 974848 | tf_op jit(solution)/shard_map/all_gather | solution.py:26
  28.5 0.2 reshape.44
  28.7 14.8 %convolution_bitcast_fusion = f32[2,64,1152]{2,1,0:T(8,128)S(1)} fusion(bf16[64,7168,1]{1,0,2:T(8,128)(2,1)S(1)} %reshape.44, bf16[2,1152,7168]{2,1,0:T(8,128)(2,1)} %param.11), kind=kOutput, calls=%fused_computation | convolution fusion | flops 2113929216 | bytes 34537472 | tf_op jit(solution)/shard_map/rd,gfd->grf/dot_general | solution.py:15
  43.5 0.0 copy-start.1
  43.5 0.0 copy-start.2
  43.5 0.0 copy-start.3
  43.5 0.1 fusion.1
  43.6 1.7 %stack.5 = bf16[16,64,1152]{2,1,0:T(8,128)(2,1)} broadcast(bf16[64,1152]{1,0:T(8,128)(2,1)S(1)} %fusion.1), dimensions={1,2} | broadcast | bytes 2506752 | tf_op jit(solution)/shard_map/stack | solution.py:29
  45.4 3.7 %all-to-all-start = ((bf16[16,64,1152]{2,1,0:T(8,128)(2,1)}), bf16[16,64,1152]{2,1,0:T(8,128)(2,1)S(1)}, u32[]{:S(2)}, u32[]{:S(2)}) async-start(bf16[16,64,1152]{2,1,0:T(8,128)(2,1)} %stack.5), calls=%async_computation | async-start | bytes 4718592 | tf_op jit(solution)/shard_map/all_to_all | solution.py:29
  49.8 44.8 %all-to-all-done = bf16[16,64,1152]{2,1,0:T(8,128)(2,1)S(1)} async-done(((bf16[16,64,1152]{2,1,0:T(8,128)(2,1)}), bf16[16,64,1152]{2,1,0:T(8,128)(2,1)S(1)}, u32[]{:S(2)}, u32[]{:S(2)}) %all-to-all-start) | async-done | bytes 2359328 | tf_op jit(solution)/shard_map/all_to_all | solution.py:29
  94.6 0.0 copy-start
  94.6 1.4 %copy-done = bf16[16,64,1152]{2,1,0:T(8,128)(2,1)} copy-done((bf16[16,64,1152]{2,1,0:T(8,128)(2,1)}, bf16[16,64,1152]{2,1,0:T(8,128)(2,1)S(1)}, u32[]{:S(2)}) %copy-start) | copy-done | bytes 2359320
  96.0 2.0 %copy.13 = bf16[16,8,8,1152]{3,2,0,1:T(8,128)(2,1)S(1)} copy(bf16[16,8,8,1152]{3,2,1,0:T(8,128)(2,1)} %bitcast.18) | data formatting | bytes 4718592 | tf_op jit(solution)/shard_map/reshape | solution.py:28
  98.0 10.5 %convolution_convert_fusion = bf16[64,448]{1,0:T(8,128)(2,1)S(1)} fusion(bf16[64,18432]{1,0:T(8,128)(2,1)S(1)} %bitcast.17, bf16[18432,448]{0,1:T(8,128)(2,1)} %param.12), kind=kOutput, calls=%fused_computation.1 | convolution fusion | flops 1056993280 | bytes 18931712 | tf_op jit(solution)/shard_map/dot_general | solution.py:27
  108.5 0.6 all_to_all.14
  109.2 12.2 %all-to-all-start.1 = ((bf16[16,4,448]{2,1,0:T(4,128)(2,1)}), bf16[16,4,448]{2,1,0:T(4,128)(2,1)S(1)}, u32[]{:S(2)}, u32[]{:S(2)}) async-start(bf16[16,4,448]{2,1,0:T(4,128)(2,1)} %all_to_all.14), calls=%async_computation.1 | async-start | bytes 131072 | tf_op jit(solution)/shard_map/all_to_all | solution.py:34
  121.4 6.9 %all-to-all-done.1 = bf16[16,4,448]{2,1,0:T(4,128)(2,1)S(1)} async-done(((bf16[16,4,448]{2,1,0:T(4,128)(2,1)}), bf16[16,4,448]{2,1,0:T(4,128)(2,1)S(1)}, u32[]{:S(2)}, u32[]{:S(2)}) %all-to-all-start.1) | async-done | bytes 57376 | tf_op jit(solution)/shard_map/all_to_all | solution.py:34
  128.4 0.1 reshape.41
  128.5 0.0 copy-done.1
  128.5 0.0 copy-done.2
  128.5 0.2 multiply_reduce_fusion
  128.7 0.0 copy-done.3
  128.7 0.8 select_convert_fusion
  (5 shorter events, 0.1 us)
Async XLA Ops:
  43.5 85.0 %copy-start.1 = (bf16[4,7168]{1,0:T(4,128)(2,1)S(1)}, bf16[4,7168]{1,0:T(4,128)(2,1)}, u32[]{:S(2)}) copy-start(bf16[4,7168]{1,0:T(4,128)(2,1)} %param.8) | copy-start | bytes 172036
  43.5 85.0 %copy-start.2 = (bf16[4,7168]{1,0:T(4,128)(2,1)S(1)}, bf16[4,7168]{1,0:T(4,128)(2,1)}, u32[]{:S(2)}) copy-start(bf16[4,7168]{1,0:T(4,128)(2,1)} %param.9) | copy-start | bytes 172036
  43.5 85.2 %copy-start.3 = (f32[7168]{0:T(1024)S(1)}, f32[7168]{0:T(1024)}, u32[]{:S(2)}) copy-start(f32[7168]{0:T(1024)} %param.13) | copy-start | bytes 86020
  45.4 49.2 %all-to-all-start = ((bf16[16,64,1152]{2,1,0:T(8,128)(2,1)}), bf16[16,64,1152]{2,1,0:T(8,128)(2,1)S(1)}, u32[]{:S(2)}, u32[]{:S(2)}) async-start(bf16[16,64,1152]{2,1,0:T(8,128)(2,1)} %stack.5), calls=%async_computation | async-start | bytes 4718592 | tf_op jit(solution)/shard_map/all_to_all | solution.py:29
  94.6 1.4 %copy-start = (bf16[16,64,1152]{2,1,0:T(8,128)(2,1)}, bf16[16,64,1152]{2,1,0:T(8,128)(2,1)S(1)}, u32[]{:S(2)}) copy-start(bf16[16,64,1152]{2,1,0:T(8,128)(2,1)S(1)} %all-to-all-done) | copy-start | bytes 7077892
  109.2 19.1 %all-to-all-start.1 = ((bf16[16,4,448]{2,1,0:T(4,128)(2,1)}), bf16[16,4,448]{2,1,0:T(4,128)(2,1)S(1)}, u32[]{:S(2)}, u32[]{:S(2)}) async-start(bf16[16,4,448]{2,1,0:T(4,128)(2,1)} %all_to_all.14), calls=%async_computation.1 | async-start | bytes 131072 | tf_op jit(solution)/shard_map/all_to_all | solution.py:34
